TPU v7x, 32 devices: a whole 2x2x4 slice. The times are simulated.
32 devices in a mesh: row: 16 (over z, x, core), feat: 2 (over y).
Axes of the slice: x: 2, y: 2, z: 4, core: 2. Of those that a mesh axis runs over, the one named last changes fastest.
Arguments:
- bin_index: int32 [1024, 49152], P('feat', 'row'), may hold values from 0 to 63
- gradient: bfloat16 [32, 49152], P(None, ('row', 'feat')), may hold values from -6 to 6
- hessian: bfloat16 [49152], P(('row', 'feat')), may hold values from 0.25 to 4
- row_node: int32 [49152], P('row'), may hold values from 0 to 7
Outputs:
- split_gain: float32 [1024, 512], P(('feat', 'row'))
- best_gain: float32 [8], replicated
All inputs are finite; a program needn't handle non-finite values.
Results may differ from a plain program's by a relative error of at most 0.0003.
Values may be sent and summed in bfloat16 or wider, within the bound.
A program may use at most 128 MiB of HBM per device.

v0:
```python
import functools
import math

import jax
import jax.numpy as jnp
from jax import lax
from jax.experimental import pallas as pl
from jax.experimental.pallas import tpu as pltpu
from jax.sharding import PartitionSpec as P

BINS = 64
NODES = 8
GROUP = 4
CHUNKS = 2

ridge_term = 1.0


def gain_kernel(outputs_count, bins_ref, rows_ref, gain_ref, masked_ref, sums_ref):
    step = pl.program_id(0)
    features = bins_ref.shape[1]
    subs, width = rows_ref.shape[1], rows_ref.shape[3]
    group = math.gcd(features, GROUP)
    columns = group * BINS
    channels = outputs_count + 1

    for sub in range(subs):
        block = rows_ref[0, sub].astype(jnp.float32)
        nodes = block[channels : channels + 1]
        levels = lax.broadcasted_iota(jnp.int32, (NODES, 1), 0).astype(jnp.float32)
        picked = nodes == levels
        masked = jnp.concatenate(
            [jnp.where(picked, block[k : k + 1], 0.0) for k in range(channels)], 0
        )
        masked_ref[:, sub * width : (sub + 1) * width] = masked.astype(jnp.bfloat16)

    masked = masked_ref[...]
    levels = lax.broadcasted_iota(jnp.int32, (BINS, 1), 0).astype(jnp.bfloat16)
    one, zero = jnp.bfloat16(1), jnp.bfloat16(0)
    for g in range(features // group):
        below = jnp.concatenate(
            [
                jnp.where(bins_ref[0, g * group + j : g * group + j + 1, :] <= levels, one, zero)
                for j in range(group)
            ],
            0,
        )
        part = lax.dot_general(
            masked, below, (((1,), (1,)), ((), ())), preferred_element_type=jnp.float32
        )
        where = slice(g * columns, (g + 1) * columns)

        @pl.when(step == 0)
        def _():
            sums_ref[:, where] = part

        @pl.when(step > 0)
        def _():
            sums_ref[:, where] += part

    @pl.when(step == pl.num_programs(0) - 1)
    def _():
        for g in range(features // group):
            where = slice(g * columns, (g + 1) * columns)
            left2 = right2 = whole2 = 0.0
            for k in range(channels):
                left = sums_ref[k * NODES : (k + 1) * NODES, where]
                whole = sums_ref[k * NODES : (k + 1) * NODES, BINS - 1 : BINS]
                right = whole - left
                if k < outputs_count:
                    left2 = left2 + left * left
                    right2 = right2 + right * right
                    whole2 = whole2 + whole * whole
            gain_ref[:, where] = (0.5 / outputs_count) * (
                left2 / (left + ridge_term)
                + right2 / (right + ridge_term)
                - whole2 / (whole + ridge_term)
            )


def chunk_gain(bins, rows, outputs_count):
    shards, features, shard_rows = bins.shape
    subs, width = rows.shape[1], rows.shape[3]
    sums_rows = (outputs_count + 1) * NODES
    flops = 2 * sums_rows * features * BINS * shards * shard_rows
    return pl.pallas_call(
        functools.partial(gain_kernel, outputs_count),
        out_shape=jax.ShapeDtypeStruct((NODES, features * BINS), jnp.float32),
        grid=(shards,),
        in_specs=[
            pl.BlockSpec((1, features, shard_rows), lambda i: (i, 0, 0)),
            pl.BlockSpec((1, subs, rows.shape[2], width), lambda i: (i, 0, 0, 0)),
        ],
        out_specs=pl.BlockSpec((NODES, features * BINS), lambda i: (0, 0)),
        scratch_shapes=[
            pltpu.VMEM((sums_rows, shard_rows), jnp.bfloat16),
            pltpu.VMEM((sums_rows, features * BINS), jnp.float32),
        ],
        compiler_params=pltpu.CompilerParams(
            dimension_semantics=("arbitrary",), vmem_limit_bytes=32 * 1024 * 1024
        ),
        cost_estimate=pl.CostEstimate(
            flops=flops, bytes_accessed=2 * (bins.size + rows.size), transcendentals=0
        ),
        name="chunk_gain",
    )(bins, rows)


def on_device(bin_index, gradient, hessian, row_node):
    shards, subs = lax.axis_size("row"), lax.axis_size("feat")
    owned = bin_index.shape[0] // shards
    outputs_count, width = gradient.shape
    shard_rows = bin_index.shape[1]
    nodes = lax.dynamic_slice_in_dim(row_node, lax.axis_index("feat") * width, width, 0)
    mine = jnp.concatenate(
        [gradient, hessian[None], nodes[None].astype(jnp.bfloat16)], 0
    )
    rows = lax.all_gather(mine, ("row", "feat"), axis=0, tiled=False)
    rows = rows.reshape(shards, subs, outputs_count + 2, width)

    chunks = math.gcd(CHUNKS, max(owned // GROUP, 1))
    span = owned // chunks
    bins = bin_index.reshape(shards, owned, shard_rows)
    gains = []
    for c in range(chunks):
        part = bins[:, c * span : (c + 1) * span].astype(jnp.bfloat16)
        part = lax.all_to_all(part, "row", 0, 0)
        gains.append(chunk_gain(part, rows, outputs_count))
    gain = jnp.concatenate(gains, 1)
    best_gain = lax.pmax(jnp.max(gain, axis=1), ("row", "feat"))
    split_gain = gain.reshape(NODES, owned, BINS).transpose(1, 0, 2)
    return (split_gain.reshape(owned, NODES * BINS), best_gain)


def solution(mesh):
    in_specs = (P("feat", "row"), P(None, ("row", "feat")), P(("row", "feat")), P("row"))
    out_specs = (P(("feat", "row"), None), P())
    return jax.shard_map(
        on_device, mesh=mesh, in_specs=in_specs, out_specs=out_specs, check_vma=False
    )
```

profile of v0, /device:TPU:0, one launch (start us, length us, event | category | flops | bytes accessed | tf_op | source)
XLA Modules:
  0.0 280.2 jit_solution(6647180913604106240)
XLA Ops:
  7.2 0.0 all-gather.4.cloned.1.call-start
  7.2 0.8 dynamic-slice_convert_fusion
  8.0 0.7 broadcast_in_dim.4
  8.7 1.6 maximum_bitcast_fusion
  10.3 0.0 all-gather.4.cloned.1.call-update
  10.3 3.5 %convert.5 = bf16[512,3072]{1,0:T(8,128)(2,1)S(1)} convert(s32[512,3072]{1,0:T(8,128)} %param.4) | non-fusion elementwise | flops 1572864 | bytes 9437184 | tf_op jit(solution)/shard_map/convert.1
  13.8 1.4 fusion
  15.2 51.3 %all_to_all.10.bins_ref = bf16[16,16,3072]{2,1,0:T(8,128)(2,1)S(1)} all-to-all(bf16[16,16,3072]{2,1,0:T(8,128)(2,1)S(1)} %get-tuple-element.3), channel_id=1, replica_groups=mesh['row'=16,'feat'=2] {'row'}, dimensions={0} | all-to-all | bytes 3145728 | tf_op jit(solution)/shard_map/all_to_all | solution.py:127
  66.5 7.0 %all-to-all-start = ((bf16[16,16,3072]{2,1,0:T(8,128)(2,1)}), bf16[16,16,3072]{2,1,0:T(8,128)(2,1)S(1)}, u32[]{:S(2)}, u32[]{:S(2)}) async-start(bf16[16,16,3072]{2,1,0:T(8,128)(2,1)} %get-tuple-element.2), calls=%async_computation | async-start | bytes 3145728 | tf_op jit(solution)/shard_map/all_to_all | solution.py:127
  73.6 19.4 %all-gather.4.cloned.1.call-done = bf16[32,34,1536]{2,1,0:T(8,128)(2,1)} async-done(((bf16[1,34,1536]{2,1,0:T(8,128)(2,1)}), bf16[32,34,1536]{2,1,0:T(8,128)(2,1)}) %all-gather.4.cloned.1.call-update) | async-done | bytes 3342352 | tf_op jit(solution)/shard_map/all_gather | solution.py:118
  93.0 0.0 copy-start
  93.0 2.1 copy-done
  95.1 69.1 %chunk_gain.3 = f32[8,1024]{1,0:T(8,128)S(1)} custom-call(bf16[16,16,3072]{2,1,0:T(8,128)(2,1)S(1)} %all_to_all.10.bins_ref, bf16[16,2,34,1536]{3,2,1,0:T(8,128)(2,1)S(1)} %bitcast.5), custom_call_target="tpu_custom_call" | custom-call | flops 26575110144 | bytes 4915200 | tf_op jit(solution)/shard_map/chunk_gain/pallas_call | solution.py:86
  164.2 0.0 all-to-all-done.bins_ref
  164.2 0.0 copy-start.1
  164.2 2.1 copy-done.1
  166.3 69.1 %chunk_gain.2 = f32[8,1024]{1,0:T(8,128)S(1)} custom-call(bf16[16,16,3072]{2,1,0:T(8,128)(2,1)S(1)} %all-to-all-done.bins_ref, bf16[16,2,34,1536]{3,2,1,0:T(8,128)(2,1)S(1)} %bitcast.6), custom_call_target="tpu_custom_call" | custom-call | flops 26575110144 | bytes 4915200 | tf_op jit(solution)/shard_map/chunk_gain/pallas_call | solution.py:86
  235.4 0.1 reduce_max.14
  235.6 0.1 reduce_max.18
  235.7 0.1 reshape.19
  235.8 0.1 copy.7
  235.9 0.7 reshape.20
  236.6 36.8 %pmax.7 = f32[8]{0:T(128)} all-reduce(f32[8]{0:T(128)S(1)} %reduce_max.19), channel_id=1, replica_groups=mesh['row'=16,'feat'=2] {'row','feat'}, use_global_device_ids=true, to_apply=%region_2.3 | all-reduce | flops 8 | bytes 64 | tf_op jit(solution)/shard_map/pmax | solution.py:130
  (3 shorter events, 0.0 us)
Async XLA Ops:
  7.2 85.8 %all-gather.4.cloned.1.call-start = ((), (), s32[]{:S(2)}) async-start(), calls=%async_computation.2 | async-start | bytes 4055040 | tf_op jit(solution)/shard_map/all_gather | solution.py:118
  66.5 97.7 %all-to-all-start = ((bf16[16,16,3072]{2,1,0:T(8,128)(2,1)}), bf16[16,16,3072]{2,1,0:T(8,128)(2,1)S(1)}, u32[]{:S(2)}, u32[]{:S(2)}) async-start(bf16[16,16,3072]{2,1,0:T(8,128)(2,1)} %get-tuple-element.2), calls=%async_computation | async-start | bytes 3145728 | tf_op jit(solution)/shard_map/all_to_all | solution.py:127
  93.0 2.1 copy-start
  164.2 2.1 copy-start.1
Sparse Core Ops, SparseCore 0:
  10.9 82.0 all-gather.3
where the time goes:
time: 281 us; the launch traced here: 280 us
  Pallas kernels  138 us (49%)
  blocking collectives  88.1 us (31%)
  waiting for transfers between devices  19.5 us (7%)
  between operations  14.1 us (5%)
  local copies, waits for them, and re-layouts  7.19 us (3%)
  starting transfers between devices  7.07 us (3%)
  other arithmetic  6.12 us (2%)
    pallas_call x2, Pallas kernels, chunk_gain(): pl.pallas_call(functools.partial(gain_kernel, outputs_count), out_shape=j...  138 us
    all_to_all x1, blocking collectives, on_device(): part = lax.all_to_all(part, 'row', 0, 0)  51.3 us
    pmax x1, blocking collectives, on_device(): best_gain = lax.pmax(jnp.max(gain, axis=1), ('row', 'feat'))  36.8 us
    all_gather x1, waiting for transfers between devices, on_device(): rows = lax.all_gather(mine, ('row', 'feat'), axis=0, tiled=False)  19.4 us
    all_to_all x1, starting transfers between devices, on_device(): part = lax.all_to_all(part, 'row', 0, 0)  7.04 us
  transfers between devices with their start and end apart: 2, of which 1 were waited for; matrix products, arithmetic and copies ran while one was open for 2% of the time, Pallas kernels for 25%

commit v1 on v0

v1 whole, which is shorter than its diff:
```python
import functools
import math

import jax
import jax.numpy as jnp
from jax import lax
from jax.experimental import pallas as pl
from jax.experimental.pallas import tpu as pltpu
from jax.sharding import PartitionSpec as P

BINS = 64
NODES = 8
GROUP = 8
PLANE = 4
LANES = 128
MESH = pl.DeviceIdType.MESH

ridge_term = 1.0


def flip(index, step, size):
    out, bit = 0, 1
    while bit < size:
        out = out + ((index // bit + step // bit) % 2) * bit
        bit *= 2
    return out


def send_plan(rows, plane):
    near = [t for t in range(plane, rows) if t % plane < plane // 2]
    far = [t for t in range(plane, rows) if t % plane >= plane // 2]
    first = near[: len(near) // 2 + 1]
    late = [t for t in near if t not in first] + far
    plan = {-1: list(range(1, plane)) + first}
    for i, t in enumerate(late):
        plan.setdefault(min(i, t - 1), []).append(t)
    return plan


def kernel(
    sizes,
    bins_ref,
    mine_ref,
    gain_ref,
    best_ref,
    raw,
    sent,
    got,
    stats,
    masked,
    sums,
    top,
    tops,
    load_sem,
    bin_send,
    bin_recv,
    stat_send,
    stat_recv,
    top_send,
    top_recv,
):
    rows, feats, plane, outputs_count, width = sizes
    owned, shard_rows = got.shape[1], got.shape[2]
    group = math.gcd(owned, GROUP)
    span = math.gcd(owned, 2 * group)
    columns = group * BINS
    planes = rows // plane
    r, y = lax.axis_index("row"), lax.axis_index("feat")

    def device(step, turn):
        return {"row": flip(r, step, rows), "feat": (y + turn) % feats}

    def load(t):
        d = flip(r, t, rows)
        return pltpu.make_async_copy(
            bins_ref.at[pl.ds(pl.multiple_of(d * owned, owned), owned)], raw.at[t], load_sem.at[t]
        )

    def bins_copy(t):
        return pltpu.make_async_remote_copy(
            src_ref=sent.at[t],
            dst_ref=got.at[t],
            send_sem=bin_send.at[t],
            recv_sem=bin_recv.at[t],
            device_id=device(t, 0),
            device_id_type=MESH,
        )

    def stat_copy(src, out_slot, in_slot, step, turn):
        return pltpu.make_async_remote_copy(
            src_ref=src,
            dst_ref=stats.at[in_slot],
            send_sem=stat_send.at[out_slot],
            recv_sem=stat_recv.at[in_slot],
            device_id=device(step, turn),
            device_id_type=MESH,
        )

    beside = [(i, v) for v in range(feats) for i in range(plane) if (i, v) != (0, 0)]

    def spread(src, base):
        for i, v in beside:
            stat_copy(
                src, (base + i) * feats + v, (base + i) * feats + (feats - v) % feats, i, v
            ).start()

    for t in range(rows):
        load(t).start()

    barrier = pltpu.get_barrier_semaphore()
    partners = [(t, 0) for t in range(1, rows)]
    partners += [(i, v) for v in range(1, feats) for i in range(plane)]
    for t, v in partners:
        pl.semaphore_signal(barrier, inc=1, device_id=device(t, v), device_id_type=MESH)

    def convert(t, _):
        load(t).wait()
        sent[t] = raw[t].astype(jnp.float32).astype(jnp.bfloat16)
        return 0

    lax.fori_loop(1, rows, convert, 0)
    load(0).wait()
    got[0] = raw[0].astype(jnp.float32).astype(jnp.bfloat16)
    stats[0] = mine_ref[...]
    sums[...] = jnp.zeros_like(sums)
    pl.semaphore_wait(barrier, len(partners))

    for p in range(1, planes):
        stat_copy(mine_ref, p * plane * feats, p * plane * feats, p * plane, 0).start()
    spread(mine_ref, 0)
    plan = send_plan(rows, plane)
    for t in plan[-1]:
        bins_copy(t).start()

    bin_levels = lax.broadcasted_iota(jnp.int32, (BINS, 1), 0).astype(jnp.bfloat16)
    node_levels = lax.broadcasted_iota(jnp.int32, (NODES, 1), 0).astype(jnp.float32)
    one, zero = jnp.bfloat16(1), jnp.bfloat16(0)
    tiles = width // LANES

    def step_of(t, _):
        @pl.when(t < planes - 1)
        def _():
            base = (t + 1) * plane
            slot = base * feats
            stat_copy(mine_ref, slot, slot, 0, 0).wait_recv()
            spread(stats.at[slot], base)

        for at, leaving in plan.items():
            if at >= 0:

                @pl.when(t == at)
                def _():
                    for other in leaving:
                        bins_copy(other).start()

        @pl.when(t > 0)
        def _():
            bins_copy(t).wait_recv()

        for u in range(feats):

            @pl.when((t % plane) + u > 0)
            def _():
                slot = t * feats + u
                stat_copy(mine_ref, slot, slot, 0, 0).wait_recv()

        for c in range(feats):
            chunk = stats.at[t * feats + (c + feats - y) % feats]
            extra = chunk[:, width : width + LANES]
            hess = jnp.concatenate([extra[j : j + 1] for j in range(tiles)], 1)
            node = jnp.concatenate([extra[tiles + j : tiles + j + 1] for j in range(tiles)], 1)
            grads = chunk[:, :width]
            where = slice(c * width, (c + 1) * width)
            for n in range(NODES):
                masked[n * outputs_count : (n + 1) * outputs_count, where] = jnp.where(
                    node == jnp.bfloat16(n), grads, zero
                )
            masked[NODES * outputs_count :, where] = jnp.where(
                node.astype(jnp.float32) == node_levels, hess.astype(jnp.float32), 0.0
            ).astype(jnp.bfloat16)

        def groups(trip, _):
            bins = got[t, pl.ds(pl.multiple_of(trip * span, span), span), :]
            for h in range(span // group):
                below = jnp.concatenate(
                    [
                        jnp.where(bins[j : j + 1] <= bin_levels, one, zero)
                        for j in range(h * group, (h + 1) * group)
                    ],
                    0,
                )
                sums[trip * (span // group) + h] += lax.dot_general(
                    masked[...], below, (((1,), (1,)), ((), ())), preferred_element_type=jnp.float32
                )
            return 0

        lax.fori_loop(0, owned // span, groups, 0)
        return 0

    lax.fori_loop(0, rows, step_of, 0)

    whole = sums[0, :, BINS - 1 : BINS]
    most = None
    for g in range(owned // group):
        lefts, rights, wholes = [], [], []
        for n in range(NODES):
            part = slice(n * outputs_count, (n + 1) * outputs_count)
            left = sums[g, part, :]
            right = whole[part] - left
            lefts.append(jnp.sum(left * left, 0, keepdims=True))
            rights.append(jnp.sum(right * right, 0, keepdims=True))
            wholes.append(jnp.sum(whole[part] * whole[part], 0, keepdims=True))
        left_hess = sums[g, NODES * outputs_count :, :]
        whole_hess = whole[NODES * outputs_count :]
        gain = (0.5 / outputs_count) * (
            jnp.concatenate(lefts, 0) / (left_hess + ridge_term)
            + jnp.concatenate(rights, 0) / (whole_hess - left_hess + ridge_term)
            - jnp.concatenate(wholes, 0) / (whole_hess + ridge_term)
        )
        gain_ref[:, g * columns : (g + 1) * columns] = gain
        for k in range(columns // LANES):
            tile = gain[:, k * LANES : (k + 1) * LANES]
            most = tile if most is None else jnp.maximum(most, tile)

    def top_copy(src, slot, step, turn, back):
        return pltpu.make_async_remote_copy(
            src_ref=top.at[src],
            dst_ref=tops.at[back],
            send_sem=top_send.at[slot],
            recv_sem=top_recv.at[back],
            device_id=device(step, turn),
            device_id_type=MESH,
        )

    top[0] = most
    across = [(rows + v, v, rows + feats - v) for v in range(1, feats)]
    for slot, v, back in across:
        top_copy(0, slot, 0, v, back).start()
    for slot, v, back in across:
        top_copy(0, slot, 0, v, slot).wait_recv()
        most = jnp.maximum(most, tops[slot])
    top[1] = most
    for t in range(1, rows):
        top_copy(1, t, t, 0, t).start()
    for t in range(1, rows):
        top_copy(1, t, t, 0, t).wait_recv()
        most = jnp.maximum(most, tops[t])
    best_ref[...] = jnp.broadcast_to(jnp.max(most, axis=1, keepdims=True), best_ref.shape)

    def drain_bins(t, _):
        bins_copy(t).wait_send()
        top_copy(1, t, t, 0, t).wait_send()
        return 0

    lax.fori_loop(1, rows, drain_bins, 0)
    for slot, v, back in across:
        top_copy(0, slot, 0, v, back).wait_send()

    def drain_stats(slot, _):
        stat_copy(mine_ref, slot, slot, 0, 0).wait_send()
        return 0

    lax.fori_loop(1, rows * feats, drain_stats, 0)


def on_device(bin_index, gradient, hessian, row_node):
    rows, feats = lax.axis_size("row"), lax.axis_size("feat")
    plane = math.gcd(rows, PLANE)
    owned = bin_index.shape[0] // rows
    outputs_count, width = gradient.shape
    shard_rows = bin_index.shape[1]
    channels = outputs_count + 1
    group = math.gcd(owned, GROUP)
    tiles = width // LANES
    nodes = lax.dynamic_slice_in_dim(row_node, lax.axis_index("feat") * width, width, 0)
    extra = jnp.concatenate(
        [hessian.reshape(tiles, LANES), nodes.astype(jnp.bfloat16).reshape(tiles, LANES)], 0
    )
    extra = jnp.pad(extra, ((0, outputs_count - 2 * tiles), (0, 0)))
    mine = jnp.concatenate([gradient, extra], 1)
    sizes = (rows, feats, plane, outputs_count, width)
    flops = 2 * channels * NODES * owned * BINS * rows * shard_rows
    vmem = pl.BlockSpec(memory_space=pltpu.VMEM)
    dma = pltpu.SemaphoreType.DMA
    gain, best = pl.pallas_call(
        functools.partial(kernel, sizes),
        out_shape=(
            jax.ShapeDtypeStruct((NODES, owned * BINS), jnp.float32),
            jax.ShapeDtypeStruct((NODES, LANES), jnp.float32),
        ),
        in_specs=[pl.BlockSpec(memory_space=pl.ANY), vmem],
        out_specs=(vmem, vmem),
        scratch_shapes=[
            pltpu.VMEM((rows, owned, shard_rows), jnp.int32),
            pltpu.VMEM((rows, owned, shard_rows), jnp.bfloat16),
            pltpu.VMEM((rows, owned, shard_rows), jnp.bfloat16),
            pltpu.VMEM((rows * feats, outputs_count, width + LANES), jnp.bfloat16),
            pltpu.VMEM((channels * NODES, shard_rows), jnp.bfloat16),
            pltpu.VMEM((owned // group, channels * NODES, group * BINS), jnp.float32),
            pltpu.VMEM((2, NODES, LANES), jnp.float32),
            pltpu.VMEM((rows + feats, NODES, LANES), jnp.float32),
            dma((rows,)),
            dma((rows,)),
            dma((rows,)),
            dma((rows * feats,)),
            dma((rows * feats,)),
            dma((rows + feats,)),
            dma((rows + feats,)),
        ],
        compiler_params=pltpu.CompilerParams(
            collective_id=1, has_side_effects=True, vmem_limit_bytes=56 * 1024 * 1024
        ),
        cost_estimate=pl.CostEstimate(
            flops=flops, bytes_accessed=4 * bin_index.size, transcendentals=0
        ),
        name="split_gains",
    )(bin_index, mine)
    split_gain = gain.reshape(NODES, owned, BINS).transpose(1, 0, 2)
    return (split_gain.reshape(owned, NODES * BINS), best[:, 0])


def solution(mesh):
    in_specs = (P("feat", "row"), P(None, ("row", "feat")), P(("row", "feat")), P("row"))
    out_specs = (P(("feat", "row"), None), P())
    return jax.shard_map(
        on_device, mesh=mesh, in_specs=in_specs, out_specs=out_specs, check_vma=False
    )
```

time: 281 us -> 117 us (0.42)
  blocking collectives: 88.1 us -> 0 us
  Pallas kernels: 138 us -> 110 us
  waiting for transfers between devices: 19.5 us -> 0 us
  between operations: 14.1 us -> 0.65 us
  starting transfers between devices: 7.07 us -> 0 us
  local copies, waits for them, and re-layouts: 7.19 us -> 3.03 us
  other arithmetic: 6.12 us -> 3.02 us
    all_to_all x1 -> x0, blocking collectives: 51.3 us -> none  [on_device(): part = lax.all_to_all(part, 'row', 0, 0)]
    pmax x1 -> x0, blocking collectives: 36.8 us -> none  [on_device(): best_gain = lax.pmax(jnp.max(gain, axis=1), ('row', 'feat'))]
    pallas_call x2 -> x1, Pallas kernels: 138 us -> 110 us  [on_device(): pl.pallas_call(functools.partial(kernel, sizes), out_shape=(jax.ShapeDtyp...]
    all_gather x1 -> x0, waiting for transfers between devices: 19.4 us -> none  [on_device(): rows = lax.all_gather(mine, ('row', 'feat'), axis=0, tiled=False)]
    all_to_all x1 -> x0, starting transfers between devices: 7.04 us -> none  [on_device(): part = lax.all_to_all(part, 'row', 0, 0)]
    unnamed x4 -> x0, local copies, waits for them, and re-layouts: 4.22 us -> none
    another operation x1 -> x0, other arithmetic: 3.5 us -> none
  transfers between devices with their start and end apart: 2 -> 0, of which waited for: 1 -> 0; matrix products, arithmetic and copies ran while one was open for 2% -> 0% of each run, Pallas kernels for 25% -> 0%
where the time goes in v1:
time: 117 us
  Pallas kernels  110 us (94%)
  local copies, waits for them, and re-layouts  3.03 us (3%)
  other arithmetic  3.02 us (3%)
    pallas_call x1, Pallas kernels, on_device(): pl.pallas_call(functools.partial(kernel, sizes), out_shape=(jax.ShapeDtyp...  110 us

profile of v1, /device:TPU:0, one launch (start us, length us, event | category | flops | bytes accessed | tf_op | source)
XLA Modules:
  0.0 116.8 jit_solution(10234092018145668399)
XLA Ops:
  0.6 0.8 fusion.3
  1.4 0.7 fusion.2
  2.1 1.5 %pad_maximum_fusion.mine_ref = bf16[32,1664]{1,0:T(8,128)(2,1)} fusion(bf16[32,128]{1,0:T(8,128)(2,1)S(1)} %fusion.2, bf16[32,1536]{1,0:T(8,128)(2,1)} %param.5), kind=kLoop, calls=%fused_computation | loop fusion | flops 212992 | bytes 212992 | tf_op jit(solution)/shard_map/concatenate | solution.py:280
  3.7 110.1 %split_gains.1 = (f32[8,2048]{1,0:T(8,128)}, f32[8,128]{1,0:T(8,128)}) custom-call(s32[512,3072]{1,0:T(8,128)} %bins_ref.1, bf16[32,1664]{1,0:T(8,128)(2,1)} %pad_maximum_fusion.mine_ref), custom_call_target="tpu_custom_call" | custom-call | flops 53150220288 | bytes 6291456 | tf_op jit(solution)/shard_map/split_gains/pallas_call | solution.py:285
  113.8 1.3 %slice_reduce_fusion = f32[8]{0:T(128)} fusion(f32[8,128]{1,0:T(8,128)} %get-tuple-element.5), kind=kLoop, calls=%fused_computation.7 | loop fusion | bytes 64 | tf_op jit(solution)/shard_map/slice | solution.py:319
  115.1 0.9 reshape.18
  116.0 0.1 copy.7
  116.1 0.7 reshape.19

commit v2 on v1

v2 whole, which is shorter than its diff:
```python
import functools
import math

import jax
import jax.numpy as jnp
from jax import lax
from jax.experimental import pallas as pl
from jax.experimental.pallas import tpu as pltpu
from jax.sharding import PartitionSpec as P

BINS = 64
NODES = 8
GROUP = 8
PLANE = 4
LANES = 128
MESH = pl.DeviceIdType.MESH

ridge_term = 1.0


def flip(index, step, size):
    out, bit = 0, 1
    while bit < size:
        out = out + ((index // bit + step // bit) % 2) * bit
        bit *= 2
    return out


def send_plan(rows, plane):
    plan = {-1: list(range(1, plane))}
    for t in range(plane, rows):
        ring, close = t // plane, t % plane < max(plane // 2, 1)
        at = max(ring - 3, -1 if ring < 3 else 0) if close else 2 * ring - 1
        plan.setdefault(at, []).append(t)
    return plan


def kernel(
    sizes,
    bins_ref,
    grad_ref,
    hess_ref,
    node_ref,
    gain_ref,
    best_ref,
    raw,
    sent,
    got,
    stats,
    masked_even,
    masked_odd,
    sums,
    top,
    tops,
    load_sem,
    bin_send,
    bin_recv,
    stat_send,
    stat_recv,
    top_send,
    top_recv,
):
    rows, feats, plane, outputs_count, width = sizes
    owned, shard_rows = got.shape[1], got.shape[2]
    group = math.gcd(owned, GROUP)
    columns = group * BINS
    half, tiles = outputs_count // 2, width // LANES
    planes = rows // plane
    r, y = lax.axis_index("row"), lax.axis_index("feat")

    def device(step, turn):
        return {"row": flip(r, step, rows), "feat": (y + turn) % feats}

    def load(t):
        d = flip(r, t, rows)
        return pltpu.make_async_copy(
            bins_ref.at[pl.ds(pl.multiple_of(d * owned, owned), owned)], raw.at[t], load_sem.at[t]
        )

    def bins_copy(t):
        return pltpu.make_async_remote_copy(
            src_ref=sent.at[t],
            dst_ref=got.at[t],
            send_sem=bin_send.at[t],
            recv_sem=bin_recv.at[t],
            device_id=device(t, 0),
            device_id_type=MESH,
        )

    def stat_copy(src, out_slot, in_slot, step, turn):
        return pltpu.make_async_remote_copy(
            src_ref=src,
            dst_ref=stats.at[in_slot],
            send_sem=stat_send.at[out_slot],
            recv_sem=stat_recv.at[in_slot],
            device_id=device(step, turn),
            device_id_type=MESH,
        )

    pair = 2 - plane % 2
    beside = [(i, v) for v in range(feats) for i in range(0, plane, pair) if (i, v) != (0, 0)]

    def spread(src, base):
        for i, v in beside:
            stat_copy(
                src, (base + i) * feats + v, (base + i) * feats + (feats - v) % feats, i, v
            ).start()

    def share(src, slot):
        stat_copy(src, slot + feats, slot + feats, 1, 0).start()

    for t in range(rows):
        load(t).start()

    stats[0, :, :width] = grad_ref[...]
    stats[0, :, width:] = jnp.zeros((outputs_count, LANES), jnp.bfloat16)
    stats[0, :tiles, width:] = hess_ref[...]
    held = node_ref[:tiles]
    for c in range(1, feats):
        held = jnp.where(y == c, node_ref[c * tiles : (c + 1) * tiles], held)
    stats[0, half : half + tiles, width:] = held.astype(jnp.float32).astype(jnp.bfloat16)

    barrier = pltpu.get_barrier_semaphore()
    partners = [(t, 0) for t in range(1, rows)]
    partners += [(t, v) for v in range(1, feats) for t in range(rows)]
    for t, v in partners:
        pl.semaphore_signal(barrier, inc=1, device_id=device(t, v), device_id_type=MESH)

    plan = send_plan(rows, plane)
    early = max(plan[-1]) + 1

    def convert(t, _):
        load(t).wait()
        sent[t] = raw[t].astype(jnp.float32).astype(jnp.bfloat16)
        return 0

    pl.semaphore_wait(barrier, len(partners))
    for p in range(1, planes):
        stat_copy(stats.at[0], p * plane * feats, p * plane * feats, p * plane, 0).start()
    spread(stats.at[0], 0)
    if pair == 2:
        share(stats.at[0], 0)
    lax.fori_loop(1, early, convert, 0)
    for t in plan[-1]:
        bins_copy(t).start()
    load(0).wait()
    got[0] = raw[0].astype(jnp.float32).astype(jnp.bfloat16)
    lax.fori_loop(early, rows, convert, 0)
    sums[...] = jnp.zeros_like(sums)

    bin_levels = lax.broadcasted_iota(jnp.int32, (BINS, 1), 0).astype(jnp.bfloat16)
    node_levels = lax.broadcasted_iota(jnp.int32, (NODES, 1), 0).astype(jnp.float32)
    one, zero = jnp.bfloat16(1), jnp.bfloat16(0)

    def arrive(t):
        for u in range(feats):
            slot = t * feats + u

            @pl.when((t % plane) + u > 0)
            def _():
                stat_copy(stats.at[0], slot, slot, 0, 0).wait_recv()

            if pair == 2:

                @pl.when((t % 2 == 0) & (t + u > 0))
                def _():
                    share(stats.at[slot], slot)

    def mask(t, masked):
        for c in range(feats):
            chunk = stats.at[t * feats + (c + feats - y) % feats]
            extra = chunk[:, width : width + LANES]
            hess = jnp.concatenate([extra[j : j + 1] for j in range(tiles)], 1)
            node = jnp.concatenate([extra[half + j : half + j + 1] for j in range(tiles)], 1)
            grads = chunk[:, :width]
            where = slice(c * width, (c + 1) * width)
            for n in range(NODES):
                masked[n * outputs_count : (n + 1) * outputs_count, where] = jnp.where(
                    node == jnp.bfloat16(n), grads, zero
                )
            masked[NODES * outputs_count :, where] = jnp.where(
                node.astype(jnp.float32) == node_levels, hess.astype(jnp.float32), 0.0
            ).astype(jnp.bfloat16)

    def shard_of(t):
        rest = planes - 2
        if plane != PLANE or rest < 1:
            return t
        i, c = t // 2, t % 2
        late = 1 - (4 // (i + 1) + 3) // 4
        j = i + 4 * rest - 4
        return 2 * (i * (1 - late) + late * (4 + 2 * (j % rest) + j // rest - 4)) + c

    def step_of(t, masked, following):
        for p in range(1, planes):

            @pl.when(t == 2 * (p - 1))
            def _():
                slot = p * plane * feats
                stat_copy(stats.at[0], slot, slot, 0, 0).wait_recv()
                spread(stats.at[slot], p * plane)

        for at, leaving in plan.items():
            if at >= 0:

                @pl.when(t == at)
                def _():
                    for other in leaving:
                        bins_copy(other).start()

        @pl.when(t < rows - 1)
        def _():
            arrive(shard_of(t + 1))

        shard = shard_of(t)

        @pl.when(t > 0)
        def _():
            bins_copy(shard).wait_recv()

        mask(shard_of((t + 1) % rows), following)
        for g in range(owned // group):
            below = jnp.concatenate(
                [
                    jnp.where(got[shard, j : j + 1, :] <= bin_levels, one, zero)
                    for j in range(g * group, (g + 1) * group)
                ],
                0,
            )
            sums[g] += lax.dot_general(
                masked[...], below, (((1,), (1,)), ((), ())), preferred_element_type=jnp.float32
            )

    def two_steps(i, _):
        step_of(2 * i, masked_even, masked_odd)
        step_of(2 * i + 1, masked_odd, masked_even)
        return 0

    arrive(0)
    mask(0, masked_even)
    lax.fori_loop(0, rows // 2, two_steps, 0)

    whole = sums[0, :, BINS - 1 : BINS]
    most = None
    for g in range(owned // group):
        lefts, rights, wholes = [], [], []
        for n in range(NODES):
            part = slice(n * outputs_count, (n + 1) * outputs_count)
            left = sums[g, part, :]
            right = whole[part] - left
            lefts.append(jnp.sum(left * left, 0, keepdims=True))
            rights.append(jnp.sum(right * right, 0, keepdims=True))
            wholes.append(jnp.sum(whole[part] * whole[part], 0, keepdims=True))
        left_hess = sums[g, NODES * outputs_count :, :]
        whole_hess = whole[NODES * outputs_count :]
        gain = (0.5 / outputs_count) * (
            jnp.concatenate(lefts, 0) / (left_hess + ridge_term)
            + jnp.concatenate(rights, 0) / (whole_hess - left_hess + ridge_term)
            - jnp.concatenate(wholes, 0) / (whole_hess + ridge_term)
        )
        gain_ref[:, g * columns : (g + 1) * columns] = gain
        for k in range(columns // LANES):
            tile = gain[:, k * LANES : (k + 1) * LANES]
            most = tile if most is None else jnp.maximum(most, tile)

    def top_copy(t, v):
        back = t * feats + (feats - v) % feats
        return pltpu.make_async_remote_copy(
            src_ref=top,
            dst_ref=tops.at[back],
            send_sem=top_send.at[t * feats + v],
            recv_sem=top_recv.at[back],
            device_id=device(t, v),
            device_id_type=MESH,
        )

    top[...] = most
    for t, v in partners:
        top_copy(t, v).start()
    for t, v in partners:
        top_copy(t, (feats - v) % feats).wait_recv()
        most = jnp.maximum(most, tops[t * feats + v])
    most = jnp.broadcast_to(jnp.max(most, axis=1, keepdims=True), most.shape)
    across = lax.broadcasted_iota(jnp.int32, most.shape, 1)
    down = lax.broadcasted_iota(jnp.int32, most.shape, 0)
    best_ref[...] = jnp.sum(jnp.where(across == down, most, 0.0), 0, keepdims=True)[:, :NODES]

    def drain_bins(t, _):
        bins_copy(t).wait_send()
        return 0

    lax.fori_loop(1, rows, drain_bins, 0)
    for t, v in partners:
        top_copy(t, v).wait_send()

    def drain_stats(slot, _):
        stat_copy(stats.at[0], slot, slot, 0, 0).wait_send()
        return 0

    lax.fori_loop(1, rows * feats, drain_stats, 0)


def on_device(bin_index, gradient, hessian, row_node):
    rows, feats = lax.axis_size("row"), lax.axis_size("feat")
    plane = math.gcd(rows, PLANE)
    owned = bin_index.shape[0] // rows
    outputs_count, width = gradient.shape
    shard_rows = bin_index.shape[1]
    channels = outputs_count + 1
    group = math.gcd(owned, GROUP)
    sizes = (rows, feats, plane, outputs_count, width)
    flops = 2 * channels * NODES * owned * BINS * rows * shard_rows
    vmem = pl.BlockSpec(memory_space=pltpu.VMEM)
    dma = pltpu.SemaphoreType.DMA
    gain, best = pl.pallas_call(
        functools.partial(kernel, sizes),
        out_shape=(
            jax.ShapeDtypeStruct((NODES, owned * BINS), jnp.float32),
            jax.ShapeDtypeStruct((1, NODES), jnp.float32),
        ),
        in_specs=[pl.BlockSpec(memory_space=pl.ANY), vmem, vmem, vmem],
        out_specs=(vmem, vmem),
        scratch_shapes=[
            pltpu.VMEM((rows, owned, shard_rows), jnp.int32),
            pltpu.VMEM((rows, owned, shard_rows), jnp.bfloat16),
            pltpu.VMEM((rows, owned, shard_rows), jnp.bfloat16),
            pltpu.VMEM((rows * feats, outputs_count, width + LANES), jnp.bfloat16),
            pltpu.VMEM((channels * NODES, shard_rows), jnp.bfloat16),
            pltpu.VMEM((channels * NODES, shard_rows), jnp.bfloat16),
            pltpu.VMEM((owned // group, channels * NODES, group * BINS), jnp.float32),
            pltpu.VMEM((NODES, LANES), jnp.float32),
            pltpu.VMEM((rows * feats, NODES, LANES), jnp.float32),
            dma((rows,)),
            dma((rows,)),
            dma((rows,)),
            dma((rows * feats,)),
            dma((rows * feats,)),
            dma((rows * feats,)),
            dma((rows * feats,)),
        ],
        compiler_params=pltpu.CompilerParams(
            collective_id=1, has_side_effects=True, vmem_limit_bytes=56 * 1024 * 1024
        ),
        cost_estimate=pl.CostEstimate(
            flops=flops, bytes_accessed=4 * bin_index.size, transcendentals=0
        ),
        name="split_gains",
    )(bin_index, gradient, hessian.reshape(-1, LANES), row_node.reshape(-1, LANES))
    split_gain = gain.reshape(NODES, owned, BINS).transpose(1, 0, 2)
    return (split_gain.reshape(owned, NODES * BINS), best[0])


def solution(mesh):
    in_specs = (P("feat", "row"), P(None, ("row", "feat")), P(("row", "feat")), P("row"))
    out_specs = (P(("feat", "row"), None), P())
    return jax.shard_map(
        on_device, mesh=mesh, in_specs=in_specs, out_specs=out_specs, check_vma=False
    )
```

time: 117 us -> 103 us (0.88)
  Pallas kernels: 110 us -> 99.7 us
  other arithmetic: 3.02 us -> 0 us
    pallas_call x1, Pallas kernels: 110 us -> 99.7 us  [on_device(): pl.pallas_call(functools.partial(kernel, sizes), out_shape=(jax.ShapeDtyp...]
    concatenate x2 -> x0, other arithmetic: 2.23 us -> none  [the longest x1 1.54 us: on_device(): mine = jnp.concatenate([gradient, extra], 1)]
    slice x1 -> x0, local copies, waits for them, and re-layouts: 1.31 us -> none  [on_device(): return (split_gain.reshape(owned, NODES * BINS), best[:, 0])]
where the time goes in v2:
time: 103 us
  Pallas kernels  99.7 us (97%)
  local copies, waits for them, and re-layouts  2.85 us (3%)
    pallas_call x1, Pallas kernels, on_device(): pl.pallas_call(functools.partial(kernel, sizes), out_shape=(jax.ShapeDtyp...  99.7 us

profile of v2, /device:TPU:0, one launch (start us, length us, event | category | flops | bytes accessed | tf_op | source)
XLA Modules:
  0.0 103.2 jit_solution(12147253762667896752)
XLA Ops:
  0.6 99.7 %split_gains.1 = (f32[8,2048]{1,0:T(8,128)}, f32[1,8]{1,0:T(1,128)}) custom-call(s32[512,3072]{1,0:T(8,128)} %bins_ref.1, bf16[32,1536]{1,0:T(8,128)(2,1)} %grad_ref.1, bf16[12,128]{1,0:T(8,128)(2,1)} %bitcast.6, s32[24,128]{1,0:T(8,128)} %bitcast.5), custom_call_target="tpu_custom_call" | custom-call | flops 53150220288 | bytes 6291456 | tf_op jit(solution)/shard_map/split_gains/pallas_call | solution.py:315
  100.3 0.9 reshape.18
  101.3 0.1 copy.6
  101.4 0.7 reshape.19
  102.1 1.1 %copy.8 = f32[8]{0:T(128)} copy(f32[8]{0:T(128)} %bitcast.7) | data formatting | bytes 64

commit v3 on v2

--- a/solution.py
+++ b/solution.py
@@ -33,6 +33,10 @@
         at = max(ring - 3, -1 if ring < 3 else 0) if close else 2 * ring - 1
         plan.setdefault(at, []).append(t)
     return plan
+
+
+def parts_of(owned):
+    return 2 if owned % 32 == 0 else 1
 
 
 def kernel(
@@ -57,12 +61,14 @@
     bin_recv,
     stat_send,
     stat_recv,
+    relay_send,
     top_send,
     top_recv,
 ):
     rows, feats, plane, outputs_count, width = sizes
     owned, shard_rows = got.shape[1], got.shape[2]
     group = math.gcd(owned, GROUP)
+    parts = parts_of(owned)
     columns = group * BINS
     half, tiles = outputs_count // 2, width // LANES
     planes = rows // plane
@@ -77,15 +83,20 @@
             bins_ref.at[pl.ds(pl.multiple_of(d * owned, owned), owned)], raw.at[t], load_sem.at[t]
         )
 
-    def bins_copy(t):
+    def bins_copy(t, h):
+        piece = pl.ds(h * (owned // parts), owned // parts)
         return pltpu.make_async_remote_copy(
-            src_ref=sent.at[t],
-            dst_ref=got.at[t],
-            send_sem=bin_send.at[t],
-            recv_sem=bin_recv.at[t],
+            src_ref=sent.at[t, piece],
+            dst_ref=got.at[t, piece],
+            send_sem=bin_send.at[t * parts + h],
+            recv_sem=bin_recv.at[t * parts + h],
             device_id=device(t, 0),
             device_id_type=MESH,
         )
+
+    def send_bins(t):
+        for h in range(parts):
+            bins_copy(t, h).start()
 
     def stat_copy(src, out_slot, in_slot, step, turn):
         return pltpu.make_async_remote_copy(
@@ -109,7 +120,10 @@
     def share(src, slot):
         stat_copy(src, slot + feats, slot + feats, 1, 0).start()
 
-    for t in range(rows):
+    plan = send_plan(rows, plane)
+    first = sorted(plan[-1], key=lambda t: (t < plane, t))
+    rest = [t for t in range(1, rows) if t not in first]
+    for t in first + [0] + rest:
         load(t).start()
 
     stats[0, :, :width] = grad_ref[...]
@@ -126,26 +140,44 @@
     for t, v in partners:
         pl.semaphore_signal(barrier, inc=1, device_id=device(t, v), device_id_type=MESH)
 
-    plan = send_plan(rows, plane)
-    early = max(plan[-1]) + 1
-
     def convert(t, _):
         load(t).wait()
         sent[t] = raw[t].astype(jnp.float32).astype(jnp.bfloat16)
         return 0
 
+    def relay(p):
+        slot = p * plane * feats
+        return pltpu.make_async_remote_copy(
+            src_ref=stats.at[0],
+            dst_ref=stats.at[slot],
+            send_sem=relay_send.at[p],
+            recv_sem=stat_recv.at[slot],
+            device_id=device(p * plane, 0),
+            device_id_type=MESH,
+        )
+
+    def wait_ring(p):
+        slot = p * plane * feats
+        stat_copy(stats.at[0], slot, slot, 0, 0).wait_recv()
+
     pl.semaphore_wait(barrier, len(partners))
     for p in range(1, planes):
-        stat_copy(stats.at[0], p * plane * feats, p * plane * feats, p * plane, 0).start()
+        relay(p).start()
     spread(stats.at[0], 0)
     if pair == 2:
         share(stats.at[0], 0)
-    lax.fori_loop(1, early, convert, 0)
-    for t in plan[-1]:
-        bins_copy(t).start()
+    ahead = [t for t in first if t < plane]
+    for i, t in enumerate(ahead):
+        convert(t, 0)
+        if i > 0:
+            send_bins(ahead[i - 1])
     load(0).wait()
     got[0] = raw[0].astype(jnp.float32).astype(jnp.bfloat16)
-    lax.fori_loop(early, rows, convert, 0)
+    send_bins(ahead[-1])
+    for t in first[: -len(ahead)] + rest:
+        convert(t, 0)
+    for t in first[: -len(ahead)]:
+        send_bins(t)
     sums[...] = jnp.zeros_like(sums)
 
     bin_levels = lax.broadcasted_iota(jnp.int32, (BINS, 1), 0).astype(jnp.bfloat16)
@@ -196,9 +228,8 @@
 
             @pl.when(t == 2 * (p - 1))
             def _():
-                slot = p * plane * feats
-                stat_copy(stats.at[0], slot, slot, 0, 0).wait_recv()
-                spread(stats.at[slot], p * plane)
+                wait_ring(p)
+                spread(stats.at[p * plane * feats], p * plane)
 
         for at, leaving in plan.items():
             if at >= 0:
@@ -206,7 +237,7 @@
                 @pl.when(t == at)
                 def _():
                     for other in leaving:
-                        bins_copy(other).start()
+                        send_bins(other)
 
         @pl.when(t < rows - 1)
         def _():
@@ -216,10 +247,16 @@
 
         @pl.when(t > 0)
         def _():
-            bins_copy(shard).wait_recv()
+            bins_copy(shard, 0).wait_recv()
 
         mask(shard_of((t + 1) % rows), following)
         for g in range(owned // group):
+            if g > 0 and g * group % (owned // parts) == 0:
+
+                @pl.when(t > 0)
+                def _():
+                    bins_copy(shard, g * group // (owned // parts)).wait_recv()
+
             below = jnp.concatenate(
                 [
                     jnp.where(got[shard, j : j + 1, :] <= bin_levels, one, zero)
@@ -258,7 +295,8 @@
             + jnp.concatenate(rights, 0) / (whole_hess - left_hess + ridge_term)
             - jnp.concatenate(wholes, 0) / (whole_hess + ridge_term)
         )
-        gain_ref[:, g * columns : (g + 1) * columns] = gain
+        for j in range(group):
+            gain_ref[:, g * group + j, :] = gain[:, j * BINS : (j + 1) * BINS]
         for k in range(columns // LANES):
             tile = gain[:, k * LANES : (k + 1) * LANES]
             most = tile if most is None else jnp.maximum(most, tile)
@@ -274,30 +312,37 @@
             device_id_type=MESH,
         )
 
+    most = jnp.broadcast_to(jnp.max(most, axis=1, keepdims=True), most.shape)
+    across = lax.broadcasted_iota(jnp.int32, most.shape, 1)
+    down = lax.broadcasted_iota(jnp.int32, most.shape, 0)
+    most = jnp.sum(jnp.where(across == down, most, 0.0), 0, keepdims=True)
     top[...] = most
-    for t, v in partners:
+    for t, v in sorted(partners, reverse=True):
         top_copy(t, v).start()
     for t, v in partners:
         top_copy(t, (feats - v) % feats).wait_recv()
         most = jnp.maximum(most, tops[t * feats + v])
-    most = jnp.broadcast_to(jnp.max(most, axis=1, keepdims=True), most.shape)
-    across = lax.broadcasted_iota(jnp.int32, most.shape, 1)
-    down = lax.broadcasted_iota(jnp.int32, most.shape, 0)
-    best_ref[...] = jnp.sum(jnp.where(across == down, most, 0.0), 0, keepdims=True)[:, :NODES]
+    best_ref[...] = most[:, :NODES]
 
     def drain_bins(t, _):
-        bins_copy(t).wait_send()
+        for h in range(parts):
+            bins_copy(t, h).wait_send()
         return 0
 
     lax.fori_loop(1, rows, drain_bins, 0)
     for t, v in partners:
         top_copy(t, v).wait_send()
 
-    def drain_stats(slot, _):
-        stat_copy(stats.at[0], slot, slot, 0, 0).wait_send()
-        return 0
-
-    lax.fori_loop(1, rows * feats, drain_stats, 0)
+    for i, v in beside:
+        for p in range(planes):
+            slot = (p * plane + i) * feats + v
+            stat_copy(stats.at[0], slot, slot, 0, 0).wait_send()
+    if pair == 2:
+        for t in range(1, rows, 2):
+            for u in range(feats):
+                stat_copy(stats.at[0], t * feats + u, t * feats + u, 0, 0).wait_send()
+    for p in range(1, planes):
+        relay(p).wait_send()
 
 
 def on_device(bin_index, gradient, hessian, row_node):
@@ -315,7 +360,7 @@
     gain, best = pl.pallas_call(
         functools.partial(kernel, sizes),
         out_shape=(
-            jax.ShapeDtypeStruct((NODES, owned * BINS), jnp.float32),
+            jax.ShapeDtypeStruct((NODES, owned, BINS), jnp.float32),
             jax.ShapeDtypeStruct((1, NODES), jnp.float32),
         ),
         in_specs=[pl.BlockSpec(memory_space=pl.ANY), vmem, vmem, vmem],
@@ -328,13 +373,14 @@
             pltpu.VMEM((channels * NODES, shard_rows), jnp.bfloat16),
             pltpu.VMEM((channels * NODES, shard_rows), jnp.bfloat16),
             pltpu.VMEM((owned // group, channels * NODES, group * BINS), jnp.float32),
-            pltpu.VMEM((NODES, LANES), jnp.float32),
-            pltpu.VMEM((rows * feats, NODES, LANES), jnp.float32),
+            pltpu.VMEM((1, LANES), jnp.float32),
+            pltpu.VMEM((rows * feats, 1, LANES), jnp.float32),
             dma((rows,)),
-            dma((rows,)),
-            dma((rows,)),
+            dma((rows * parts_of(owned),)),
+            dma((rows * parts_of(owned),)),
             dma((rows * feats,)),
             dma((rows * feats,)),
+            dma((rows // plane,)),
             dma((rows * feats,)),
             dma((rows * feats,)),
         ],
@@ -346,7 +392,7 @@
         ),
         name="split_gains",
     )(bin_index, gradient, hessian.reshape(-1, LANES), row_node.reshape(-1, LANES))
-    split_gain = gain.reshape(NODES, owned, BINS).transpose(1, 0, 2)
+    split_gain = gain.transpose(1, 0, 2)
     return (split_gain.reshape(owned, NODES * BINS), best[0])
 
 

time: 103 us -> 101 us (0.981)
  Pallas kernels: 99.7 us -> 97.4 us
    pallas_call x1, Pallas kernels: 99.7 us -> 97.4 us  [on_device(): pl.pallas_call(functools.partial(kernel, sizes), out_shape=(jax.ShapeDtyp...]
where the time goes in v3:
time: 101 us
  Pallas kernels  97.4 us (96%)
  local copies, waits for them, and re-layouts  2.88 us (3%)
    pallas_call x1, Pallas kernels, on_device(): pl.pallas_call(functools.partial(kernel, sizes), out_shape=(jax.ShapeDtyp...  97.4 us

profile of v3, /device:TPU:0, one launch (start us, length us, event | category | flops | bytes accessed | tf_op | source)
XLA Modules:
  0.0 100.9 jit_solution(16396286770463517050)
XLA Ops:
  0.6 97.4 %split_gains.1 = (f32[8,32,64]{2,1,0:T(8,128)}, f32[1,8]{1,0:T(1,128)}) custom-call(s32[512,3072]{1,0:T(8,128)} %bins_ref.1, bf16[32,1536]{1,0:T(8,128)(2,1)} %grad_ref.1, bf16[12,128]{1,0:T(8,128)(2,1)} %bitcast.6, s32[24,128]{1,0:T(8,128)} %bitcast.5), custom_call_target="tpu_custom_call" | custom-call | flops 53150220288 | bytes 6291456 | tf_op jit(solution)/shard_map/split_gains/pallas_call | solution.py:360
  98.0 1.0 copy.6
  99.0 0.7 reshape.15
  99.7 1.2 %copy.8 = f32[8]{0:T(128)} copy(f32[8]{0:T(128)} %bitcast.7) | data formatting | bytes 64
